TPU v7x, 32 devices: a whole 2x2x4 slice. The times are simulated.
32 devices in a mesh: seq: 16 (over z, x, core), tp: 2 (over y).
Axes of the slice: x: 2, y: 2, z: 4, core: 2. Of those that a mesh axis runs over, the one named last changes fastest.
Arguments:
- hidden_in: bfloat16 [2048, 4096], P('seq', 'tp'), may hold values from -64 to 64
- span_order: int32 [16], replicated, may hold values from 0 to 15, each once
- norm_gain: bfloat16 [4096], P('tp'), may hold values from 0.099609375 to 1.8984375
- w_query: bfloat16 [4096, 4096], P('seq', 'tp'), may hold values from -0.09375 to 0.09375
- bias_query: bfloat16 [4096], P('tp'), may hold values from -14 to 14
- key_value_weight: bfloat16 [4096, 2, 1024], P('seq', None, 'tp'), may hold values from -0.09375 to 0.09375
- bias_kv: bfloat16 [2, 1024], P(None, 'tp'), may hold values from -14 to 14
- w_out: bfloat16 [4096, 4096], P('tp', 'seq'), may hold values from -0.09375 to 0.09375
- post_gain: bfloat16 [4096], P('tp'), may hold values from 0.099609375 to 1.8984375
Outputs:
- attn_out: bfloat16 [2048, 4096], P('seq', 'tp')
- normed: bfloat16 [2048, 4096], P('seq', 'tp')
Inputs may be any that keep to these rules, and one draw needn't show every extreme that they name: Each span number appears once; row r of hidden_in belongs to span span_order[r // 128].
All inputs are finite; a program needn't handle non-finite values.
Results may differ from a plain program's by a relative error of at most 0.014.
Values may be sent and summed in bfloat16 or wider, within the bound.
A program may use at most 128 MiB of HBM per device.

v0:
```python
import math
import jax
import jax.numpy as jnp
from jax import lax
from jax.sharding import PartitionSpec as P

MODEL_WIDTH = 4096
HEAD_SIZE = 128
GROUP = 4
eps = 1e-06
rope_base = 1000000.0


def apply_rotary(field, token_positions):
    half = field.shape[-1] // 2
    inverse = jnp.exp(-math.log(rope_base) * jnp.arange(half, dtype=jnp.float32) / half)
    angles = token_positions.astype(jnp.float32)[:, None] * inverse[None, :]
    cosine = jnp.cos(angles)[:, None, :]
    sine = jnp.sin(angles)[:, None, :]
    first = field[..., :half]
    second = field[..., half:]
    return jnp.concatenate(
        [first * cosine - second * sine, second * cosine + first * sine], axis=-1
    )


def span_lookup(order, devices):
    table_ids = jnp.arange(order.shape[0], dtype=jnp.int32)
    return jnp.sum(jnp.where(devices[:, None] == table_ids[None, :], order[None, :], 0), axis=1)


def per_device(
    hidden_in,
    span_order,
    norm_gain,
    w_query,
    bias_query,
    key_value_weight,
    bias_kv,
    w_out,
    post_gain,
):
    tok_rows = hidden_in.shape[0]
    seq_index = lax.axis_index("seq")
    own_span = span_lookup(span_order, jnp.full((1,), seq_index, jnp.int32))[0]
    token_positions = own_span * tok_rows + jnp.arange(tok_rows, dtype=jnp.int32)
    local = hidden_in.astype(jnp.float32)
    raw_rows, gains = (
        lax.all_gather(hidden_in, "tp", axis=1, tiled=True),
        lax.all_gather(norm_gain[None, :], "tp", axis=1, tiled=True),
    )
    full_rows = raw_rows.astype(jnp.float32)
    meansq = jnp.mean(full_rows * full_rows, axis=1, keepdims=True)
    normed_in = (full_rows * lax.rsqrt(meansq + eps) * gains.astype(jnp.float32)).astype(
        jnp.bfloat16
    )
    columns = normed_in
    query_proj = jnp.dot(
        columns,
        lax.all_gather(w_query, "seq", axis=0, tiled=True),
        preferred_element_type=jnp.float32,
    )
    columns = normed_in
    pair_proj = jnp.einsum(
        "tr,rkc->tkc",
        columns,
        lax.all_gather(key_value_weight, "seq", axis=0, tiled=True),
        preferred_element_type=jnp.float32,
    )
    query_heads = w_query.shape[1] // HEAD_SIZE
    kv_heads = key_value_weight.shape[2] // HEAD_SIZE
    query_proj = query_proj + bias_query.astype(jnp.float32)[None, :]
    queries = apply_rotary(
        query_proj.reshape(tok_rows, query_heads, HEAD_SIZE), token_positions
    ).astype(jnp.bfloat16)
    pair_proj = pair_proj + bias_kv.astype(jnp.float32)[None, :, :]
    rotated_keys = apply_rotary(
        pair_proj[:, 0, :].reshape(tok_rows, kv_heads, HEAD_SIZE), token_positions
    )
    rotated_keys = rotated_keys.astype(jnp.bfloat16).reshape(tok_rows, kv_heads * HEAD_SIZE)
    value_rows = pair_proj[:, 1, :].astype(jnp.bfloat16)
    grouped = (
        queries.reshape(tok_rows, kv_heads, GROUP, HEAD_SIZE)
        .transpose(1, 2, 0, 3)
        .reshape(kv_heads, GROUP * tok_rows, HEAD_SIZE)
    )
    query_pos = jnp.tile(token_positions, GROUP)
    last_query = jnp.max(token_positions)
    scale = 1.0 / math.sqrt(HEAD_SIZE)
    start_state = (
        jnp.full((kv_heads, GROUP * tok_rows), -1e30, jnp.float32),
        jnp.zeros((kv_heads, GROUP * tok_rows), jnp.float32),
        jnp.zeros((kv_heads, GROUP * tok_rows, HEAD_SIZE), jnp.float32),
    )
    key_piece = lax.all_gather(rotated_keys, "seq", axis=0, tiled=True)
    value_piece = lax.all_gather(value_rows, "seq", axis=0, tiled=True)
    count = key_piece.shape[0]
    block = math.gcd(count, 1536)

    def visit(step, state):
        first = step * block
        key_block = lax.dynamic_slice_in_dim(key_piece, first, block, 0).reshape(
            block, kv_heads, HEAD_SIZE
        )
        value_block = lax.dynamic_slice_in_dim(value_piece, first, block, 0).reshape(
            block, kv_heads, HEAD_SIZE
        )
        row_ids = first + jnp.arange(block, dtype=jnp.int32)
        key_pos = span_lookup(span_order, row_ids // tok_rows) * tok_rows + row_ids % tok_rows

        def update(current):
            maxima, totals, sums = current
            scores = (
                jnp.einsum("kqd,nkd->kqn", grouped, key_block, preferred_element_type=jnp.float32)
                * scale
            )
            allowed = (key_pos[None, :] <= query_pos[:, None])[None, :, :]
            scores = jnp.where(allowed, scores, -1e30)
            fresh = jnp.maximum(maxima, jnp.max(scores, axis=2))
            weights = jnp.where(allowed, jnp.exp(scores - fresh[:, :, None]), 0.0)
            factor = jnp.exp(maxima - fresh)
            totals = totals * factor + jnp.sum(weights, axis=2)
            sums = sums * factor[:, :, None] + jnp.einsum(
                "kqn,nkd->kqd",
                weights.astype(jnp.bfloat16),
                value_block,
                preferred_element_type=jnp.float32,
            )
            return (fresh, totals, sums)

        return lax.cond(jnp.min(key_pos) <= last_query, update, lambda current: current, state)

    maxima, totals, sums = lax.fori_loop(0, count // block, visit, start_state)
    attended = (sums / totals[:, :, None]).astype(jnp.bfloat16)
    attended = (
        attended.reshape(kv_heads, GROUP, tok_rows, HEAD_SIZE)
        .transpose(2, 0, 1, 3)
        .reshape(tok_rows, query_heads * HEAD_SIZE)
    )
    partial_out = jnp.dot(
        attended,
        lax.all_gather(w_out, "seq", axis=1, tiled=True),
        preferred_element_type=jnp.float32,
    )
    mixed = lax.psum_scatter(
        partial_out.astype(jnp.bfloat16), "tp", scatter_dimension=1, tiled=True
    ).astype(jnp.float32)
    attn_out = mixed.astype(jnp.bfloat16)
    stream = local + mixed
    post_sq = lax.psum(jnp.sum(stream * stream, axis=1), "tp")
    normed = (
        stream
        * lax.rsqrt(post_sq / MODEL_WIDTH + eps)[:, None]
        * post_gain.astype(jnp.float32)[None, :]
    ).astype(jnp.bfloat16)
    return (attn_out, normed)


def solution(mesh):
    placed = (
        P("seq", "tp"),
        P(),
        P("tp"),
        P("seq", "tp"),
        P("tp"),
        P("seq", None, "tp"),
        P(None, "tp"),
        P("tp", "seq"),
        P("tp"),
    )
    return jax.shard_map(
        per_device,
        mesh=mesh,
        in_specs=placed,
        out_specs=(P("seq", "tp"), P("seq", "tp")),
        check_vma=False,
    )
```

profile of v0, /device:TPU:0, one launch (start us, length us, event | category | flops | bytes accessed | tf_op | source)
XLA Modules:
  0.0 499.7 jit_solution(17849845767442077635)
XLA Ops:
  7.9 1.9 copy.44
  9.9 5.5 %all-gather = bf16[4096]{0:T(1024)(128)(2,1)S(1)} all-gather(bf16[2048]{0:T(1024)(128)(2,1)} %param.15), channel_id=2, replica_groups=mesh['seq'=16,'tp'=2] {'tp'}, dimensions={0}, use_global_device_ids=true | all-gather | bytes 12288 | tf_op jit(solution)/shard_map/all_gather | solution.py:50
  16.1 17.4 %all-gather.9.cloned.1.call-done = bf16[128,4096]{1,0:T(8,128)(2,1)} async-done(((bf16[128,2048]{1,0:T(8,128)(2,1)}), bf16[128,4096]{1,0:T(8,128)(2,1)}) %all-gather.9.cloned.1.call-update) | async-done | bytes 1048592 | tf_op jit(solution)/shard_map/all_gather | solution.py:49
  33.6 1.5 fusion.18
  35.1 75.6 %all-gather.11.cloned.1.call-done = bf16[4096,2,512]{2,0,1:T(8,128)(2,1)} async-done(((bf16[256,2,512]{2,0,1:T(8,128)(2,1)}), bf16[4096,2,512]{2,0,1:T(8,128)(2,1)}) %all-gather.11.cloned.1.call-update) | async-done | bytes 8388624 | tf_op jit(solution)/shard_map/all_gather | solution.py:67
  110.7 5.0 %convolution_add_fusion.1 = f32[128,2,512]{2,0,1:T(8,128)S(1)} fusion(bf16[4096,2,512]{2,0,1:T(8,128)(2,1)} %all-gather.11.cloned.1.call-done, bf16[128,4096]{1,0:T(8,128)(2,1)} %all-gather.9.cloned.1.call-done, f32[4096]{0:T(1024)S(1)} %mul.210, f32[128]{0:T(128)S(1)} %add_rsqrt_fusion.1, f32[2,512]{1,0:T(2,128)S(1)} %convert_element_type.69), kind=kOutput, calls=%fused_computation.39 | convolution fusion | flops 1075970048 | bytes 9982464 | tf_op jit(solution)/shard_map/tr,rkc->tkc/dot_general | solution.py:64
  121.5 35.1 %all-gather.19.cloned.1.call-done = bf16[2048,1,512]{2,0,1:T(8,128)(2,1)} async-done(((bf16[128,1,512]{2,0,1:T(8,128)(2,1)}), bf16[2048,1,512]{2,0,1:T(8,128)(2,1)}) %all-gather.19.cloned.1.call-update) | async-done | bytes 2097168 | tf_op jit(solution)/shard_map/all_gather | solution.py:96
  156.6 2.9 copy.48
  159.5 124.3 %all-gather.15.cloned.1.call-done = bf16[4096,2048]{1,0:T(8,128)(2,1)} async-done(((bf16[256,2048]{1,0:T(8,128)(2,1)}), bf16[4096,2048]{1,0:T(8,128)(2,1)}) %all-gather.15.cloned.1.call-update) | async-done | bytes 16777232 | tf_op jit(solution)/shard_map/all_gather | solution.py:60
  283.8 8.2 %fusion.21 = f32[16,8,16,128]{3,1,2,0:T(8,128)S(1)} fusion(bf16[4096,2048]{1,0:T(8,128)(2,1)} %all-gather.15.cloned.1.call-done, f32[2048]{0:T(1024)S(1)} %convert_element_type.72, bf16[128,4096]{1,0:T(8,128)(2,1)S(1)} %copy-done, f32[4096]{0:T(1024)S(1)} %mul.210, f32[128]{0:T(128)S(1)} %add_rsqrt_fusion.1), kind=kOutput, calls=%fused_computation.38 | convolution fusion | flops 2149842944 | bytes 18899456 | tf_op jit(solution)/shard_map/dot_general | solution.py:58
  293.3 32.3 %all-gather.13.cloned.1.call-done = bf16[2048,512]{0,1:T(8,128)(2,1)} async-done(((bf16[128,512]{0,1:T(8,128)(2,1)}), bf16[2048,512]{0,1:T(8,128)(2,1)}) %all-gather.13.cloned.1.call-update) | async-done | bytes 2097168 | tf_op jit(solution)/shard_map/all_gather | solution.py:95
  325.6 1.1 broadcast_in_dim.105
  326.7 33.3 %while.20 = (s32[]{:T(128)}, f32[4,512]{1,0:T(4,128)S(1)}, f32[4,512]{1,0:T(4,128)S(1)}, f32[4,512,128]{2,1,0:T(8,128)}, s32[16]{0:T(128)S(1)}, /*index=5*/s32[]...) while((s32[]{:T(128)}, f32[4,512]{1,0:T(4,128)S(1)}, ...), condition=%wide.region_10.11_spmd.clone, body=%wide.region_3.10_spmd.clone.sunk | while | flops 551332864 | bytes 27935672 | solution.py:133
  328.7 6.3 %conditional.3 = ((f32[4,512]{1,0:T(4,128)S(1)}, f32[4,512]{1,0:T(4,128)S(1)}, f32[4,512,128]{2,1,0:T(8,128)})) conditional(s32[]{:T(128)} %convert_element_type.117, (f32[4,512]{1,0:T(4,128)S(1)}, f32[4,512]{1,0:T(4,128)S(1)}, f32[4,512,128]{2,1,0:T(8,128)}) %tuple.77, (s32[512]{0:T(512)S(1)}, s32[128]{0:T(128)S(1)}, s32[]{:T(128)}, ...), branch_computations={%region_6.6_spmd, %region_7.9_spmd} | conditional | flops 551292928 | bytes 27925118 | solution.py:131
  328.7 1.1 constant_dynamic-slice_fusion
  332.2 1.8 fusion.8
  337.0 6.3 %conditional.3 = ((f32[4,512]{1,0:T(4,128)S(1)}, f32[4,512]{1,0:T(4,128)S(1)}, f32[4,512,128]{2,1,0:T(8,128)})) conditional(s32[]{:T(128)} %convert_element_type.117, (f32[4,512]{1,0:T(4,128)S(1)}, f32[4,512]{1,0:T(4,128)S(1)}, f32[4,512,128]{2,1,0:T(8,128)}) %tuple.77, (s32[512]{0:T(512)S(1)}, s32[128]{0:T(128)S(1)}, s32[]{:T(128)}, ...), branch_computations={%region_6.6_spmd, %region_7.9_spmd} | conditional | flops 551292928 | bytes 27925118 | solution.py:131
  337.0 1.2 constant_dynamic-slice_fusion
  340.6 1.8 fusion.8
  345.4 6.3 %conditional.3 = ((f32[4,512]{1,0:T(4,128)S(1)}, f32[4,512]{1,0:T(4,128)S(1)}, f32[4,512,128]{2,1,0:T(8,128)})) conditional(s32[]{:T(128)} %convert_element_type.117, (f32[4,512]{1,0:T(4,128)S(1)}, f32[4,512]{1,0:T(4,128)S(1)}, f32[4,512,128]{2,1,0:T(8,128)}) %tuple.77, (s32[512]{0:T(512)S(1)}, s32[128]{0:T(128)S(1)}, s32[]{:T(128)}, ...), branch_computations={%region_6.6_spmd, %region_7.9_spmd} | conditional | flops 551292928 | bytes 27925118 | solution.py:131
  345.4 1.1 constant_dynamic-slice_fusion
  348.9 1.8 fusion.8
  353.7 6.3 %conditional.3 = ((f32[4,512]{1,0:T(4,128)S(1)}, f32[4,512]{1,0:T(4,128)S(1)}, f32[4,512,128]{2,1,0:T(8,128)})) conditional(s32[]{:T(128)} %convert_element_type.117, (f32[4,512]{1,0:T(4,128)S(1)}, f32[4,512]{1,0:T(4,128)S(1)}, f32[4,512,128]{2,1,0:T(8,128)}) %tuple.77, (s32[512]{0:T(512)S(1)}, s32[128]{0:T(128)S(1)}, s32[]{:T(128)}, ...), branch_computations={%region_6.6_spmd, %region_7.9_spmd} | conditional | flops 551292928 | bytes 27925118 | solution.py:131
  353.7 1.1 constant_dynamic-slice_fusion
  357.2 1.8 fusion.8
  360.0 1.6 divide_convert_fusion
  361.8 94.8 %all-gather.17.cloned.1.call-done = bf16[2048,4096]{1,0:T(8,128)(2,1)} async-done(((bf16[2048,256]{1,0:T(8,128)(2,1)}), bf16[2048,4096]{1,0:T(8,128)(2,1)}) %all-gather.17.cloned.1.call-update) | async-done | bytes 16777232 | tf_op jit(solution)/shard_map/all_gather | solution.py:142
  456.6 9.2 %convolution_convert_fusion = bf16[128,4096]{1,0:T(8,128)(2,1)} fusion(bf16[128,2048]{0,1:T(8,128)(2,1)S(1)} %bitcast.47, bf16[2048,4096]{1,0:T(8,128)(2,1)} %all-gather.17.cloned.1.call-done), kind=kOutput, calls=%fused_computation.31 | convolution fusion | flops 2148007936 | bytes 18350080 | tf_op jit(solution)/shard_map/dot_general | solution.py:140
  465.9 18.7 %reduce-scatter.2.cloned.1.call-done = bf16[128,2048]{1,0:T(8,128)(2,1)} async-done(((bf16[128,4096]{1,0:T(8,128)(2,1)}), bf16[128,2048]{1,0:T(8,128)(2,1)}) %reduce-scatter.2.cloned.1.call-update) | async-done | bytes 524304 | tf_op jit(solution)/shard_map/reduce_scatter | solution.py:145
  484.6 1.3 multiply_reduce_fusion
  485.9 4.9 psum.7
  490.8 2.0 multiply_convert_fusion
  (105 shorter events, 24.3 us)
Async XLA Ops:
  7.2 26.4 %all-gather.9.cloned.1.call-start = ((), (), s32[]{:S(2)}) async-start(), calls=%async_computation.1 | async-start | bytes 1572864 | tf_op jit(solution)/shard_map/all_gather | solution.py:49
  7.9 102.8 %all-gather.11.cloned.1.call-start = ((), (), s32[]{:S(2)}) async-start(), calls=%async_computation.2 | async-start | bytes 8912896 | tf_op jit(solution)/shard_map/all_gather | solution.py:67
  9.9 146.8 %all-gather.19.cloned.1.call-start = ((), (), s32[]{:S(2)}) async-start(), calls=%async_computation.7 | async-start | bytes 2228224 | tf_op jit(solution)/shard_map/all_gather | solution.py:96
  35.1 81.9 %copy-start.4 = (s32[16]{0:T(128)S(1)}, s32[16]{0:T(128)}, u32[]{:S(2)}) copy-start(s32[16]{0:T(128)} %param.14) | copy-start | bytes 196
  115.7 5.2 %copy-start.5 = (bf16[2048]{0:T(1024)(128)(2,1)S(1)}, bf16[2048]{0:T(1024)(128)(2,1)}, u32[]{:S(2)}) copy-start(bf16[2048]{0:T(1024)(128)(2,1)} %param.17) | copy-start | bytes 12292
  116.4 167.4 %all-gather.15.cloned.1.call-start = ((), (), s32[]{:S(2)}) async-start(), calls=%async_computation.4 | async-start | bytes 17825792 | tf_op jit(solution)/shard_map/all_gather | solution.py:60
  117.0 166.8 %copy-start = (bf16[128,4096]{1,0:T(8,128)(2,1)S(1)}, bf16[128,4096]{1,0:T(8,128)(2,1)}, u32[]{:S(2)}) copy-start(bf16[128,4096]{1,0:T(8,128)(2,1)} %all-gather.9.cloned.1.call-done) | copy-start | bytes 3145732
  117.0 208.7 %all-gather.13.cloned.1.call-start = ((), (), s32[]{:S(2)}) async-start(), calls=%async_computation.3 | async-start | bytes 2228224 | tf_op jit(solution)/shard_map/all_gather | solution.py:95
  120.1 336.6 %all-gather.17.cloned.1.call-start = ((), (), s32[]{:S(2)}) async-start(), calls=%async_computation.5 | async-start | bytes 17825792 | tf_op jit(solution)/shard_map/all_gather | solution.py:142
  120.7 363.9 %reduce-scatter.2.cloned.1.call-start = ((), (), s32[]{:S(2)}) async-start(), calls=%async_computation.6 | async-start | bytes 1572864 | tf_op jit(solution)/shard_map/reduce_scatter | solution.py:145
  330.1 2.1 copy-start.2
  334.0 1.0 copy-start.3
  338.4 2.1 copy-start.2
  342.4 1.0 copy-start.3
  346.8 2.1 copy-start.2
  350.7 1.0 copy-start.3
  355.1 2.1 copy-start.2
  359.0 1.0 copy-start.3
  456.6 9.2 %copy-start.6 = (bf16[2048]{0:T(1024)(128)(2,1)S(1)}, bf16[2048]{0:T(1024)(128)(2,1)}, u32[]{:S(2)}) copy-start(bf16[2048]{0:T(1024)(128)(2,1)} %param.21) | copy-start | bytes 12292
  456.6 27.9 %copy-start.1 = (bf16[128,2048]{1,0:T(8,128)(2,1)S(1)}, bf16[128,2048]{1,0:T(8,128)(2,1)}, u32[]{:S(2)}) copy-start(bf16[128,2048]{1,0:T(8,128)(2,1)} %param.13) | copy-start | bytes 1572868
Sparse Core Ops, SparseCore 0:
  9.5 23.9 all-gather.8
  36.3 74.2 all-gather.10
  116.5 40.0 all-gather.18
  158.6 125.1 all-gather.14
  286.4 39.2 all-gather.12
  327.7 128.9 all-gather.16
  466.0 18.5 reduce-scatter.1
where the time goes:
time: 500 us
  waiting for transfers between devices  400 us (80%)
  matrix products  33.6 us (7%)
  other arithmetic  18.1 us (4%)
  local copies, waits for them, and re-layouts  16.7 us (3%)
  between operations  15 us (3%)
  blocking collectives  10.4 us (2%)
  loops' own time  5.46 us (1%)
    all_gather x1, waiting for transfers between devices, per_device(): lax.all_gather(w_query, 'seq', axis=0, tiled=True)  124 us
    all_gather x1, waiting for transfers between devices, per_device(): lax.all_gather(w_out, 'seq', axis=1, tiled=True)  94.8 us
    all_gather x1, waiting for transfers between devices, per_device(): lax.all_gather(key_value_weight, 'seq', axis=0, tiled=True)  75.6 us
    all_gather x1, waiting for transfers between devices, per_device(): value_piece = lax.all_gather(value_rows, 'seq', axis=0, tiled=True)  35.1 us
    all_gather x1, waiting for transfers between devices, per_device(): key_piece = lax.all_gather(rotated_keys, 'seq', axis=0, tiled=True)  32.3 us
    reduce_scatter x1, waiting for transfers between devices, per_device(): lax.psum_scatter(partial_out.astype(jnp.bfloat16), 'tp', scatter_dimensio...  18.7 us
    all_gather x1, waiting for transfers between devices, per_device(): lax.all_gather(hidden_in, 'tp', axis=1, tiled=True)  17.4 us
  transfers between devices with their start and end apart: 7, of which 7 were waited for; matrix products, arithmetic and copies ran while one was open for 9% of the time, Pallas kernels for 0%

commit v1 on v0

--- a/solution.py
+++ b/solution.py
@@ -61,12 +61,22 @@
         preferred_element_type=jnp.float32,
     )
     columns = normed_in
-    pair_proj = jnp.einsum(
-        "tr,rkc->tkc",
-        columns,
-        lax.all_gather(key_value_weight, "seq", axis=0, tiled=True),
-        preferred_element_type=jnp.float32,
-    )
+    size, index, extent = (lax.axis_size("seq"), lax.axis_index("seq"), key_value_weight.shape[0])
+    right = [(i, (i + 1) % size) for i in range(size)]
+    held, total = (key_value_weight, None)
+    for step_2 in range(size):
+        following = lax.ppermute(held, "seq", right) if step_2 < size - 1 else None
+        update_2 = jnp.einsum(
+            "tr,rkc->tkc",
+            lax.dynamic_slice_in_dim(
+                columns, (index - step_2) % size * extent, held.shape[0], axis=1
+            ),
+            held,
+            preferred_element_type=jnp.float32,
+        )
+        total = update_2 if total is None else total + update_2
+        held = following
+    pair_proj = total
     query_heads = w_query.shape[1] // HEAD_SIZE
     kv_heads = key_value_weight.shape[2] // HEAD_SIZE
     query_proj = query_proj + bias_query.astype(jnp.float32)[None, :]

time: 500 us -> 563 us (1.13)
  waiting for transfers between devices: 400 us -> 463 us
    ppermute x0 -> x15, waiting for transfers between devices: none -> 158 us  [per_device(): following = lax.ppermute(held, 'seq', right) if step_2 < size - 1 else None]
    all_gather x1 -> x0, waiting for transfers between devices: 75.6 us -> none  [per_device(): lax.all_gather(key_value_weight, 'seq', axis=0, tiled=True)]
    all_gather x1, waiting for transfers between devices: 17.4 us -> 0.01 us  [per_device(): lax.all_gather(hidden_in, 'tp', axis=1, tiled=True)]
  transfers between devices with their start and end apart: 7 -> 21, of which waited for: 7 -> 20; matrix products, arithmetic and copies ran while one was open for 9% -> 9% of each run, Pallas kernels for 0% -> 0%
where the time goes in v1:
time: 563 us
  waiting for transfers between devices  463 us (82%)
  matrix products  32.2 us (6%)
  other arithmetic  20 us (4%)
  local copies, waits for them, and re-layouts  16 us (3%)
  between operations  15.2 us (3%)
  blocking collectives  9.43 us (2%)
  loops' own time  5.71 us (1%)
    ppermute x15, waiting for transfers between devices, per_device(): following = lax.ppermute(held, 'seq', right) if step_2 < size - 1 else None  158 us
    all_gather x1, waiting for transfers between devices, per_device(): lax.all_gather(w_query, 'seq', axis=0, tiled=True)  124 us
    all_gather x1, waiting for transfers between devices, per_device(): lax.all_gather(w_out, 'seq', axis=1, tiled=True)  94.5 us
    all_gather x1, waiting for transfers between devices, per_device(): value_piece = lax.all_gather(value_rows, 'seq', axis=0, tiled=True)  34 us
    all_gather x1, waiting for transfers between devices, per_device(): key_piece = lax.all_gather(rotated_keys, 'seq', axis=0, tiled=True)  32.4 us
    reduce_scatter x1, waiting for transfers between devices, per_device(): lax.psum_scatter(partial_out.astype(jnp.bfloat16), 'tp', scatter_dimensio...  18.7 us
  transfers between devices with their start and end apart: 21, of which 20 were waited for; matrix products, arithmetic and copies ran while one was open for 9% of the time, Pallas kernels for 0%

profile of v1, /device:TPU:0, one launch (start us, length us, event | category | flops | bytes accessed | tf_op | source)
XLA Modules:
  0.0 562.6 jit_solution(17275331197739798459)
XLA Ops:
  8.9 11.8 %collective-permute-done = bf16[256,2,512]{2,0,1:T(8,128)(2,1)S(1)} collective-permute-done((bf16[256,2,512]{2,0,1:T(8,128)(2,1)S(1)}, bf16[256,2,512]{2,0,1:T(8,128)(2,1)S(1)}, u32[]{:S(2)}, u32[]{:S(2)}) %collective-permute-start) | collective-permute-done | bytes 524320 | tf_op jit(solution)/shard_map/ppermute | solution.py:68
  20.7 11.3 %collective-permute-done.1 = bf16[256,2,512]{2,0,1:T(8,128)(2,1)S(1)} collective-permute-done((bf16[256,2,512]{2,0,1:T(8,128)(2,1)S(1)}, bf16[256,2,512]{2,0,1:T(8,128)(2,1)S(1)}, u32[]{:S(2)}, u32[]{:S(2)}) %collective-permute-start.1) | collective-permute-done | bytes 524320 | tf_op jit(solution)/shard_map/ppermute | solution.py:68
  32.0 11.3 %collective-permute-done.2 = bf16[256,2,512]{2,0,1:T(8,128)(2,1)S(1)} collective-permute-done((bf16[256,2,512]{2,0,1:T(8,128)(2,1)S(1)}, bf16[256,2,512]{2,0,1:T(8,128)(2,1)S(1)}, u32[]{:S(2)}, u32[]{:S(2)}) %collective-permute-start.2) | collective-permute-done | bytes 524320 | tf_op jit(solution)/shard_map/ppermute | solution.py:68
  43.4 11.3 %collective-permute-done.3 = bf16[256,2,512]{2,0,1:T(8,128)(2,1)S(1)} collective-permute-done((bf16[256,2,512]{2,0,1:T(8,128)(2,1)S(1)}, bf16[256,2,512]{2,0,1:T(8,128)(2,1)S(1)}, u32[]{:S(2)}, u32[]{:S(2)}) %collective-permute-start.3) | collective-permute-done | bytes 524320 | tf_op jit(solution)/shard_map/ppermute | solution.py:68
  54.8 11.2 %collective-permute-done.4 = bf16[256,2,512]{2,0,1:T(8,128)(2,1)S(1)} collective-permute-done((bf16[256,2,512]{2,0,1:T(8,128)(2,1)S(1)}, bf16[256,2,512]{2,0,1:T(8,128)(2,1)S(1)}, u32[]{:S(2)}, u32[]{:S(2)}) %collective-permute-start.4) | collective-permute-done | bytes 524320 | tf_op jit(solution)/shard_map/ppermute | solution.py:68
  66.0 11.3 %collective-permute-done.5 = bf16[256,2,512]{2,0,1:T(8,128)(2,1)S(1)} collective-permute-done((bf16[256,2,512]{2,0,1:T(8,128)(2,1)S(1)}, bf16[256,2,512]{2,0,1:T(8,128)(2,1)S(1)}, u32[]{:S(2)}, u32[]{:S(2)}) %collective-permute-start.5) | collective-permute-done | bytes 524320 | tf_op jit(solution)/shard_map/ppermute | solution.py:68
  77.3 4.5 all-gather
  84.2 4.4 collective-permute-done.6
  90.6 9.3 %collective-permute-done.7 = bf16[256,2,512]{2,0,1:T(8,128)(2,1)S(1)} collective-permute-done((bf16[256,2,512]{2,0,1:T(8,128)(2,1)S(1)}, bf16[256,2,512]{2,0,1:T(8,128)(2,1)S(1)}, u32[]{:S(2)}, u32[]{:S(2)}) %collective-permute-start.7) | collective-permute-done | bytes 524320 | tf_op jit(solution)/shard_map/ppermute | solution.py:68
  100.4 10.8 %collective-permute-done.8 = bf16[256,2,512]{2,0,1:T(8,128)(2,1)S(1)} collective-permute-done((bf16[256,2,512]{2,0,1:T(8,128)(2,1)S(1)}, bf16[256,2,512]{2,0,1:T(8,128)(2,1)S(1)}, u32[]{:S(2)}, u32[]{:S(2)}) %collective-permute-start.8) | collective-permute-done | bytes 524320 | tf_op jit(solution)/shard_map/ppermute | solution.py:68
  111.7 10.8 %collective-permute-done.9 = bf16[256,2,512]{2,0,1:T(8,128)(2,1)S(1)} collective-permute-done((bf16[256,2,512]{2,0,1:T(8,128)(2,1)S(1)}, bf16[256,2,512]{2,0,1:T(8,128)(2,1)S(1)}, u32[]{:S(2)}, u32[]{:S(2)}) %collective-permute-start.9) | collective-permute-done | bytes 524320 | tf_op jit(solution)/shard_map/ppermute | solution.py:68
  123.0 10.8 %collective-permute-done.10 = bf16[256,2,512]{2,0,1:T(8,128)(2,1)S(1)} collective-permute-done((bf16[256,2,512]{2,0,1:T(8,128)(2,1)S(1)}, bf16[256,2,512]{2,0,1:T(8,128)(2,1)S(1)}, u32[]{:S(2)}, u32[]{:S(2)}) %collective-permute-start.10) | collective-permute-done | bytes 524320 | tf_op jit(solution)/shard_map/ppermute | solution.py:68
  134.3 10.8 %collective-permute-done.11 = bf16[256,2,512]{2,0,1:T(8,128)(2,1)S(1)} collective-permute-done((bf16[256,2,512]{2,0,1:T(8,128)(2,1)S(1)}, bf16[256,2,512]{2,0,1:T(8,128)(2,1)S(1)}, u32[]{:S(2)}, u32[]{:S(2)}) %collective-permute-start.11) | collective-permute-done | bytes 524320 | tf_op jit(solution)/shard_map/ppermute | solution.py:68
  145.6 10.8 %collective-permute-done.12 = bf16[256,2,512]{2,0,1:T(8,128)(2,1)S(1)} collective-permute-done((bf16[256,2,512]{2,0,1:T(8,128)(2,1)S(1)}, bf16[256,2,512]{2,0,1:T(8,128)(2,1)S(1)}, u32[]{:S(2)}, u32[]{:S(2)}) %collective-permute-start.12) | collective-permute-done | bytes 524320 | tf_op jit(solution)/shard_map/ppermute | solution.py:68
  156.9 10.8 %collective-permute-done.13 = bf16[256,2,512]{2,0,1:T(8,128)(2,1)S(1)} collective-permute-done((bf16[256,2,512]{2,0,1:T(8,128)(2,1)S(1)}, bf16[256,2,512]{2,0,1:T(8,128)(2,1)S(1)}, u32[]{:S(2)}, u32[]{:S(2)}) %collective-permute-start.13) | collective-permute-done | bytes 524320 | tf_op jit(solution)/shard_map/ppermute | solution.py:68
  168.2 10.8 %collective-permute-done.14 = bf16[256,2,512]{2,0,1:T(8,128)(2,1)S(1)} collective-permute-done((bf16[256,2,512]{2,0,1:T(8,128)(2,1)S(1)}, bf16[256,2,512]{2,0,1:T(8,128)(2,1)S(1)}, u32[]{:S(2)}, u32[]{:S(2)}) %collective-permute-start.14) | collective-permute-done | bytes 524320 | tf_op jit(solution)/shard_map/ppermute | solution.py:68
  185.4 34.0 %all-gather.16.cloned.1.call-done = bf16[2048,1,512]{2,0,1:T(8,128)(2,1)} async-done(((bf16[128,1,512]{2,0,1:T(8,128)(2,1)}), bf16[2048,1,512]{2,0,1:T(8,128)(2,1)}) %all-gather.16.cloned.1.call-update) | async-done | bytes 2097168 | tf_op jit(solution)/shard_map/all_gather | solution.py:106
  219.3 2.9 copy.53
  222.3 124.4 %all-gather.12.cloned.1.call-done = bf16[4096,2048]{1,0:T(8,128)(2,1)} async-done(((bf16[256,2048]{1,0:T(8,128)(2,1)}), bf16[4096,2048]{1,0:T(8,128)(2,1)}) %all-gather.12.cloned.1.call-update) | async-done | bytes 16777232 | tf_op jit(solution)/shard_map/all_gather | solution.py:60
  346.7 8.1 %fusion.21 = f32[16,8,16,128]{3,1,2,0:T(8,128)S(1)} fusion(bf16[128,4096]{1,0:T(8,128)(2,1)S(1)} %fusion.20, bf16[4096,2048]{1,0:T(8,128)(2,1)} %all-gather.12.cloned.1.call-done, f32[2048]{0:T(1024)S(1)} %convert_element_type.72), kind=kOutput, calls=%fused_computation.38 | convolution fusion | flops 2147745792 | bytes 18882560 | tf_op jit(solution)/shard_map/dot_general | solution.py:58
  356.1 32.4 %all-gather.10.cloned.1.call-done = bf16[2048,512]{0,1:T(8,128)(2,1)} async-done(((bf16[128,512]{0,1:T(8,128)(2,1)}), bf16[2048,512]{0,1:T(8,128)(2,1)}) %all-gather.10.cloned.1.call-update) | async-done | bytes 2097168 | tf_op jit(solution)/shard_map/all_gather | solution.py:105
  389.6 33.5 %while.20 = (s32[]{:T(128)}, f32[4,512]{1,0:T(4,128)S(1)}, f32[4,512]{1,0:T(4,128)S(1)}, f32[4,512,128]{2,1,0:T(8,128)}, s32[16]{0:T(128)S(1)}, /*index=5*/s32[]...) while((s32[]{:T(128)}, f32[4,512]{1,0:T(4,128)S(1)}, ...), condition=%wide.region_10.11_spmd.clone, body=%wide.region_3.10_spmd.clone.sunk | while | flops 551332864 | bytes 27935680 | solution.py:143
  391.7 6.3 %conditional.3 = ((f32[4,512]{1,0:T(4,128)S(1)}, f32[4,512]{1,0:T(4,128)S(1)}, f32[4,512,128]{2,1,0:T(8,128)})) conditional(s32[]{:T(128)} %convert_element_type.109, (f32[4,512]{1,0:T(4,128)S(1)}, f32[4,512]{1,0:T(4,128)S(1)}, f32[4,512,128]{2,1,0:T(8,128)}) %tuple.77, (s32[512]{0:T(512)S(1)}, s32[128]{0:T(128)S(1)}, s32[]{:T(128)}, ...), branch_computations={%region_6.6_spmd, %region_7.9_spmd} | conditional | flops 551292928 | bytes 27925118 | solution.py:141
  395.2 1.8 fusion.8
  400.0 6.3 %conditional.3 = ((f32[4,512]{1,0:T(4,128)S(1)}, f32[4,512]{1,0:T(4,128)S(1)}, f32[4,512,128]{2,1,0:T(8,128)})) conditional(s32[]{:T(128)} %convert_element_type.109, (f32[4,512]{1,0:T(4,128)S(1)}, f32[4,512]{1,0:T(4,128)S(1)}, f32[4,512,128]{2,1,0:T(8,128)}) %tuple.77, (s32[512]{0:T(512)S(1)}, s32[128]{0:T(128)S(1)}, s32[]{:T(128)}, ...), branch_computations={%region_6.6_spmd, %region_7.9_spmd} | conditional | flops 551292928 | bytes 27925118 | solution.py:141
  408.4 6.3 %conditional.3 = ((f32[4,512]{1,0:T(4,128)S(1)}, f32[4,512]{1,0:T(4,128)S(1)}, f32[4,512,128]{2,1,0:T(8,128)})) conditional(s32[]{:T(128)} %convert_element_type.109, (f32[4,512]{1,0:T(4,128)S(1)}, f32[4,512]{1,0:T(4,128)S(1)}, f32[4,512,128]{2,1,0:T(8,128)}) %tuple.77, (s32[512]{0:T(512)S(1)}, s32[128]{0:T(128)S(1)}, s32[]{:T(128)}, ...), branch_computations={%region_6.6_spmd, %region_7.9_spmd} | conditional | flops 551292928 | bytes 27925118 | solution.py:141
  416.8 6.3 %conditional.3 = ((f32[4,512]{1,0:T(4,128)S(1)}, f32[4,512]{1,0:T(4,128)S(1)}, f32[4,512,128]{2,1,0:T(8,128)})) conditional(s32[]{:T(128)} %convert_element_type.109, (f32[4,512]{1,0:T(4,128)S(1)}, f32[4,512]{1,0:T(4,128)S(1)}, f32[4,512,128]{2,1,0:T(8,128)}) %tuple.77, (s32[512]{0:T(512)S(1)}, s32[128]{0:T(128)S(1)}, s32[]{:T(128)}, ...), branch_computations={%region_6.6_spmd, %region_7.9_spmd} | conditional | flops 551292928 | bytes 27925118 | solution.py:141
  425.0 94.5 %all-gather.14.cloned.1.call-done = bf16[2048,4096]{1,0:T(8,128)(2,1)} async-done(((bf16[2048,256]{1,0:T(8,128)(2,1)}), bf16[2048,4096]{1,0:T(8,128)(2,1)}) %all-gather.14.cloned.1.call-update) | async-done | bytes 16777232 | tf_op jit(solution)/shard_map/all_gather | solution.py:152
  519.5 9.2 %convolution_convert_fusion = bf16[128,4096]{1,0:T(8,128)(2,1)} fusion(bf16[128,2048]{0,1:T(8,128)(2,1)S(1)} %bitcast.107, bf16[2048,4096]{1,0:T(8,128)(2,1)} %all-gather.14.cloned.1.call-done), kind=kOutput, calls=%fused_computation.31 | convolution fusion | flops 2148007936 | bytes 18350080 | tf_op jit(solution)/shard_map/dot_general | solution.py:150
  528.8 18.7 %reduce-scatter.2.cloned.1.call-done = bf16[128,2048]{1,0:T(8,128)(2,1)} async-done(((bf16[128,4096]{1,0:T(8,128)(2,1)}), bf16[128,2048]{1,0:T(8,128)(2,1)}) %reduce-scatter.2.cloned.1.call-update) | async-done | bytes 524304 | tf_op jit(solution)/shard_map/reduce_scatter | solution.py:155
  548.8 4.9 psum.7
  553.7 2.0 multiply_convert_fusion
  (172 shorter events, 46.6 us)
Async XLA Ops:
  7.2 83.2 %copy-start.3 = (bf16[256,2,512]{2,1,0:T(2,128)(2,1)S(1)}, bf16[256,2,512]{2,1,0:T(2,128)(2,1)}, u32[]{:S(2)}) copy-start(bf16[256,2,512]{2,1,0:T(2,128)(2,1)} %param.18) | copy-start | bytes 1572868
  7.2 75.3 %all-gather.8.cloned.1.call-start = ((), (), s32[]{:S(2)}) async-start(), calls=%async_computation.1 | async-start | bytes 1572864 | tf_op jit(solution)/shard_map/all_gather | solution.py:49
  8.4 12.4 %collective-permute-start = (bf16[256,2,512]{2,0,1:T(8,128)(2,1)S(1)}, bf16[256,2,512]{2,0,1:T(8,128)(2,1)S(1)}, u32[]{:S(2)}, u32[]{:S(2)}) collective-permute-start(bf16[256,2,512]{2,0,1:T(8,128)(2,1)S(1)} %copy.48), channel_id=1, source_target_pairs={{0,2},{2,4},{4,6},{6,8},{8,10},{10,12},{12,14},{14,16},{16,18},{18... | collective-permute-start | bytes 1572872 | tf_op jit(solution)/shard_map/ppermute | solution.py:68
  20.7 22.6 %copy-start.4 = (bf16[256,2,512]{2,0,1:T(8,128)(2,1)}, bf16[256,2,512]{2,0,1:T(8,128)(2,1)S(1)}, u32[]{:S(2)}) copy-start(bf16[256,2,512]{2,0,1:T(8,128)(2,1)S(1)} %collective-permute-done) | copy-start | bytes 1572868
  20.7 11.3 %collective-permute-start.1 = (bf16[256,2,512]{2,0,1:T(8,128)(2,1)S(1)}, bf16[256,2,512]{2,0,1:T(8,128)(2,1)S(1)}, u32[]{:S(2)}, u32[]{:S(2)}) collective-permute-start(bf16[256,2,512]{2,0,1:T(8,128)(2,1)S(1)} %collective-permute-done), channel_id=1, source_target_pairs={{0,2},{2,4},{4,6},{6,8},{8,10},{10,12},{12,14},{14,16},{16,18},{18... | collective-permute-start | bytes 1572872 | tf_op jit(solution)/shard_map/ppermute | solution.py:68
  32.0 22.6 %copy-start.10 = (bf16[256,2,512]{2,0,1:T(8,128)(2,1)}, bf16[256,2,512]{2,0,1:T(8,128)(2,1)S(1)}, u32[]{:S(2)}) copy-start(bf16[256,2,512]{2,0,1:T(8,128)(2,1)S(1)} %collective-permute-done.1) | copy-start | bytes 1572868
  32.0 11.3 %collective-permute-start.2 = (bf16[256,2,512]{2,0,1:T(8,128)(2,1)S(1)}, bf16[256,2,512]{2,0,1:T(8,128)(2,1)S(1)}, u32[]{:S(2)}, u32[]{:S(2)}) collective-permute-start(bf16[256,2,512]{2,0,1:T(8,128)(2,1)S(1)} %collective-permute-done.1), channel_id=1, source_target_pairs={{0,2},{2,4},{4,6},{6,8},{8,10},{10,12},{12,14},{14,16},{16,18},{18... | collective-permute-start | bytes 1572872 | tf_op jit(solution)/shard_map/ppermute | solution.py:68
  43.3 11.3 %collective-permute-start.3 = (bf16[256,2,512]{2,0,1:T(8,128)(2,1)S(1)}, bf16[256,2,512]{2,0,1:T(8,128)(2,1)S(1)}, u32[]{:S(2)}, u32[]{:S(2)}) collective-permute-start(bf16[256,2,512]{2,0,1:T(8,128)(2,1)S(1)} %collective-permute-done.2), channel_id=1, source_target_pairs={{0,2},{2,4},{4,6},{6,8},{8,10},{10,12},{12,14},{14,16},{16,18},{18... | collective-permute-start | bytes 1572872 | tf_op jit(solution)/shard_map/ppermute | solution.py:68
  54.7 34.0 %copy-start.8 = (bf16[256,2,512]{2,0,1:T(8,128)(2,1)}, bf16[256,2,512]{2,0,1:T(8,128)(2,1)S(1)}, u32[]{:S(2)}) copy-start(bf16[256,2,512]{2,0,1:T(8,128)(2,1)S(1)} %collective-permute-done.3) | copy-start | bytes 1572868
  54.7 11.4 %collective-permute-start.4 = (bf16[256,2,512]{2,0,1:T(8,128)(2,1)S(1)}, bf16[256,2,512]{2,0,1:T(8,128)(2,1)S(1)}, u32[]{:S(2)}, u32[]{:S(2)}) collective-permute-start(bf16[256,2,512]{2,0,1:T(8,128)(2,1)S(1)} %collective-permute-done.3), channel_id=1, source_target_pairs={{0,2},{2,4},{4,6},{6,8},{8,10},{10,12},{12,14},{14,16},{16,18},{18... | collective-permute-start | bytes 1572872 | tf_op jit(solution)/shard_map/ppermute | solution.py:68
  54.7 164.6 %all-gather.16.cloned.1.call-start = ((), (), s32[]{:S(2)}) async-start(), calls=%async_computation.6 | async-start | bytes 2228224 | tf_op jit(solution)/shard_map/all_gather | solution.py:106
  66.0 11.3 %collective-permute-start.5 = (bf16[256,2,512]{2,0,1:T(8,128)(2,1)S(1)}, bf16[256,2,512]{2,0,1:T(8,128)(2,1)S(1)}, u32[]{:S(2)}, u32[]{:S(2)}) collective-permute-start(bf16[256,2,512]{2,0,1:T(8,128)(2,1)S(1)} %collective-permute-done.4), channel_id=1, source_target_pairs={{0,2},{2,4},{4,6},{6,8},{8,10},{10,12},{12,14},{14,16},{16,18},{18... | collective-permute-start | bytes 1572872 | tf_op jit(solution)/shard_map/ppermute | solution.py:68
  77.3 11.3 %collective-permute-start.6 = (bf16[256,2,512]{2,0,1:T(8,128)(2,1)S(1)}, bf16[256,2,512]{2,0,1:T(8,128)(2,1)S(1)}, u32[]{:S(2)}, u32[]{:S(2)}) collective-permute-start(bf16[256,2,512]{2,0,1:T(8,128)(2,1)S(1)} %collective-permute-done.5), channel_id=1, source_target_pairs={{0,2},{2,4},{4,6},{6,8},{8,10},{10,12},{12,14},{14,16},{16,18},{18... | collective-permute-start | bytes 1572872 | tf_op jit(solution)/shard_map/ppermute | solution.py:68
  82.5 17.7 %copy-start.11 = (bf16[256,2,512]{2,0,1:T(8,128)(2,1)S(1)}, bf16[256,2,512]{2,0,1:T(8,128)(2,1)}, u32[]{:S(2)}) copy-start(bf16[256,2,512]{2,0,1:T(8,128)(2,1)} %copy-done.10) | copy-start | bytes 1572868
  82.5 28.7 %copy-start.7 = (bf16[256,2,512]{2,0,1:T(8,128)(2,1)S(1)}, bf16[256,2,512]{2,0,1:T(8,128)(2,1)}, u32[]{:S(2)}) copy-start(bf16[256,2,512]{2,0,1:T(8,128)(2,1)} %copy-done.6) | copy-start | bytes 1572868
  88.6 11.3 %collective-permute-start.7 = (bf16[256,2,512]{2,0,1:T(8,128)(2,1)S(1)}, bf16[256,2,512]{2,0,1:T(8,128)(2,1)S(1)}, u32[]{:S(2)}, u32[]{:S(2)}) collective-permute-start(bf16[256,2,512]{2,0,1:T(8,128)(2,1)S(1)} %collective-permute-done.6), channel_id=1, source_target_pairs={{0,2},{2,4},{4,6},{6,8},{8,10},{10,12},{12,14},{14,16},{16,18},{18... | collective-permute-start | bytes 1572872 | tf_op jit(solution)/shard_map/ppermute | solution.py:68
  90.4 21.1 %copy-start.9 = (bf16[256,2,512]{2,0,1:T(8,128)(2,1)S(1)}, bf16[256,2,512]{2,0,1:T(8,128)(2,1)}, u32[]{:S(2)}) copy-start(bf16[256,2,512]{2,0,1:T(8,128)(2,1)} %copy-done.8) | copy-start | bytes 1572868
  90.6 32.1 %copy-start.15 = (bf16[256,2,512]{2,0,1:T(8,128)(2,1)S(1)}, bf16[256,2,512]{2,0,1:T(8,128)(2,1)}, u32[]{:S(2)}) copy-start(bf16[256,2,512]{2,0,1:T(8,128)(2,1)} %copy-done.14) | copy-start | bytes 1572868
  99.9 11.3 %collective-permute-start.8 = (bf16[256,2,512]{2,0,1:T(8,128)(2,1)S(1)}, bf16[256,2,512]{2,0,1:T(8,128)(2,1)S(1)}, u32[]{:S(2)}, u32[]{:S(2)}) collective-permute-start(bf16[256,2,512]{2,0,1:T(8,128)(2,1)S(1)} %collective-permute-done.7), channel_id=1, source_target_pairs={{0,2},{2,4},{4,6},{6,8},{8,10},{10,12},{12,14},{14,16},{16,18},{18... | collective-permute-start | bytes 1572872 | tf_op jit(solution)/shard_map/ppermute | solution.py:68
  100.2 33.7 %copy-start.13 = (bf16[256,2,512]{2,0,1:T(8,128)(2,1)S(1)}, bf16[256,2,512]{2,0,1:T(8,128)(2,1)}, u32[]{:S(2)}) copy-start(bf16[256,2,512]{2,0,1:T(8,128)(2,1)} %copy-done.12) | copy-start | bytes 1572868
  111.2 11.3 %collective-permute-start.9 = (bf16[256,2,512]{2,0,1:T(8,128)(2,1)S(1)}, bf16[256,2,512]{2,0,1:T(8,128)(2,1)S(1)}, u32[]{:S(2)}, u32[]{:S(2)}) collective-permute-start(bf16[256,2,512]{2,0,1:T(8,128)(2,1)S(1)} %collective-permute-done.8), channel_id=1, source_target_pairs={{0,2},{2,4},{4,6},{6,8},{8,10},{10,12},{12,14},{14,16},{16,18},{18... | collective-permute-start | bytes 1572872 | tf_op jit(solution)/shard_map/ppermute | solution.py:68
  122.5 11.3 %collective-permute-start.10 = (bf16[256,2,512]{2,0,1:T(8,128)(2,1)S(1)}, bf16[256,2,512]{2,0,1:T(8,128)(2,1)S(1)}, u32[]{:S(2)}, u32[]{:S(2)}) collective-permute-start(bf16[256,2,512]{2,0,1:T(8,128)(2,1)S(1)} %collective-permute-done.9), channel_id=1, source_target_pairs={{0,2},{2,4},{4,6},{6,8},{8,10},{10,12},{12,14},{14,16},{16,18},{18... | collective-permute-start | bytes 1572872 | tf_op jit(solution)/shard_map/ppermute | solution.py:68
  133.8 11.3 %collective-permute-start.11 = (bf16[256,2,512]{2,0,1:T(8,128)(2,1)S(1)}, bf16[256,2,512]{2,0,1:T(8,128)(2,1)S(1)}, u32[]{:S(2)}, u32[]{:S(2)}) collective-permute-start(bf16[256,2,512]{2,0,1:T(8,128)(2,1)S(1)} %collective-permute-done.10), channel_id=1, source_target_pairs={{0,2},{2,4},{4,6},{6,8},{8,10},{10,12},{12,14},{14,16},{16,18},{18... | collective-permute-start | bytes 1572872 | tf_op jit(solution)/shard_map/ppermute | solution.py:68
  145.1 11.3 %collective-permute-start.12 = (bf16[256,2,512]{2,0,1:T(8,128)(2,1)S(1)}, bf16[256,2,512]{2,0,1:T(8,128)(2,1)S(1)}, u32[]{:S(2)}, u32[]{:S(2)}) collective-permute-start(bf16[256,2,512]{2,0,1:T(8,128)(2,1)S(1)} %collective-permute-done.11), channel_id=1, source_target_pairs={{0,2},{2,4},{4,6},{6,8},{8,10},{10,12},{12,14},{14,16},{16,18},{18... | collective-permute-start | bytes 1572872 | tf_op jit(solution)/shard_map/ppermute | solution.py:68
  156.4 11.3 %collective-permute-start.13 = (bf16[256,2,512]{2,0,1:T(8,128)(2,1)S(1)}, bf16[256,2,512]{2,0,1:T(8,128)(2,1)S(1)}, u32[]{:S(2)}, u32[]{:S(2)}) collective-permute-start(bf16[256,2,512]{2,0,1:T(8,128)(2,1)S(1)} %collective-permute-done.12), channel_id=1, source_target_pairs={{0,2},{2,4},{4,6},{6,8},{8,10},{10,12},{12,14},{14,16},{16,18},{18... | collective-permute-start | bytes 1572872 | tf_op jit(solution)/shard_map/ppermute | solution.py:68
  156.7 24.1 %copy-start.16 = (s32[16]{0:T(128)S(1)}, s32[16]{0:T(128)}, u32[]{:S(2)}) copy-start(s32[16]{0:T(128)} %param.14) | copy-start | bytes 196
  167.7 11.3 %collective-permute-start.14 = (bf16[256,2,512]{2,0,1:T(8,128)(2,1)S(1)}, bf16[256,2,512]{2,0,1:T(8,128)(2,1)S(1)}, u32[]{:S(2)}, u32[]{:S(2)}) collective-permute-start(bf16[256,2,512]{2,0,1:T(8,128)(2,1)S(1)} %collective-permute-done.13), channel_id=1, source_target_pairs={{0,2},{2,4},{4,6},{6,8},{8,10},{10,12},{12,14},{14,16},{16,18},{18... | collective-permute-start | bytes 1572872 | tf_op jit(solution)/shard_map/ppermute | solution.py:68
  180.0 166.7 %all-gather.12.cloned.1.call-start = ((), (), s32[]{:S(2)}) async-start(), calls=%async_computation.3 | async-start | bytes 17825792 | tf_op jit(solution)/shard_map/all_gather | solution.py:60
  180.7 207.8 %all-gather.10.cloned.1.call-start = ((), (), s32[]{:S(2)}) async-start(), calls=%async_computation.2 | async-start | bytes 2228224 | tf_op jit(solution)/shard_map/all_gather | solution.py:105
  183.8 335.7 %all-gather.14.cloned.1.call-start = ((), (), s32[]{:S(2)}) async-start(), calls=%async_computation.4 | async-start | bytes 17825792 | tf_op jit(solution)/shard_map/all_gather | solution.py:152
  184.4 363.1 %reduce-scatter.2.cloned.1.call-start = ((), (), s32[]{:S(2)}) async-start(), calls=%async_computation.5 | async-start | bytes 1572864 | tf_op jit(solution)/shard_map/reduce_scatter | solution.py:155
  519.5 27.9 %copy-start = (bf16[128,2048]{1,0:T(8,128)(2,1)S(1)}, bf16[128,2048]{1,0:T(8,128)(2,1)}, u32[]{:S(2)}) copy-start(bf16[128,2048]{1,0:T(8,128)(2,1)} %param.13) | copy-start | bytes 1572868
  (14 other events, 89.7 us)
Sparse Core Ops, SparseCore 0:
  54.9 22.9 all-gather.7
  180.1 39.1 all-gather.15
  221.5 125.1 all-gather.11
  349.3 39.2 all-gather.9
  390.5 128.9 all-gather.13
  528.9 18.5 reduce-scatter.1
